TPU v7x, 32 devices: a whole 2x2x4 slice. The times are simulated.
32 devices in a mesh: seq: 4 (over y, x), sample: 2 (over core), head: 4 (over z).
Axes of the slice: x: 2, y: 2, z: 4, core: 2. Of those that a mesh axis runs over, the one named last changes fastest.
Arguments:
- block_in: bfloat16 [4, 2048, 1024], P('sample', 'seq'), may hold values from -6 to 6
- out_cotangent: bfloat16 [4, 2048, 1024], P('sample', 'seq'), may hold values from -6 to 6
- norm_gain: float32 [1024], replicated, may hold values from 0.25 to 1.75
- gate_proj: bfloat16 [1024, 2048], P(None, 'head'), may hold values from -0.296875 to 0.296875
- value_proj: bfloat16 [1024, 2048], P(None, 'head'), may hold values from -0.1875 to 0.1875
- state_proj: bfloat16 [2, 1024, 128], P(None, None, 'head'), may hold values from -0.1875 to 0.1875
- step_proj: bfloat16 [1024, 32], P(None, 'head'), may hold values from -0.1875 to 0.1875
- conv_value: float32 [4, 2048], P(None, 'head'), may hold values from -0.6 to 0.6
- conv_state: float32 [4, 2, 128], P(None, None, 'head'), may hold values from -0.6 to 0.6
- conv_value_bias: float32 [2048], P('head'), may hold values from -0.5 to 0.5
- conv_state_bias: float32 [2, 128], P(None, 'head'), may hold values from -0.5 to 0.5
- step_bias: float32 [32], P('head'), may hold values from -4.5 to -3
- decay_log: float32 [32], P('head'), may hold values from -10 to 1
- skip_gain: float32 [32], P('head'), may hold values from 0.5 to 1.5
- gated_gain: float32 [2048], P('head'), may hold values from 0.25 to 1.75
- out_proj: bfloat16 [2048, 1024], P('head'), may hold values from -0.125 to 0.125
Outputs:
- block_out: bfloat16 [4, 2048, 1024], P('sample', 'seq')
- input_grad: float32 [4, 2048, 1024], P('sample', 'seq')
- norm_gain_grad: float32 [1024], replicated
- gate_proj_grad: float32 [1024, 2048], P(None, 'head')
- value_proj_grad: float32 [1024, 2048], P(None, 'head')
- state_proj_grad: float32 [2, 1024, 128], P(None, None, 'head')
- step_proj_grad: float32 [1024, 32], P(None, 'head')
- conv_value_grad: float32 [4, 2048], P(None, 'head')
- conv_state_grad: float32 [4, 2, 128], P(None, None, 'head')
- conv_value_bias_grad: float32 [2048], P('head')
- conv_state_bias_grad: float32 [2, 128], P(None, 'head')
- step_bias_grad: float32 [32], P('head')
- decay_log_grad: float32 [32], P('head')
- skip_gain_grad: float32 [32], P('head')
- gated_gain_grad: float32 [2048], P('head')
- out_proj_grad: float32 [2048, 1024], P('head')
All inputs are finite; a program needn't handle non-finite values.
Results may differ from a plain program's by a relative error of at most 0.0055.
The roundings to bfloat16 on the way count: a program that leaves them out, or rounds other values in their place, can miss the bound.
Values may be sent and summed in bfloat16 or wider, within the bound.
A program may use at most 192 MiB of HBM per device.

v0:
```python
import jax
import jax.numpy as jnp
from jax import lax
from jax.sharding import PartitionSpec as P

GROUP = 256
highest = lax.Precision.HIGHEST


def shifted(array, axis, by):
    size = lax.axis_size(axis)
    pairs = [(i, i + by) for i in range(size) if 0 <= i + by < size]
    return lax.ppermute(array, axis, pairs)


def entering(part, axis, combine, identity, reverse):
    count = lax.axis_size(axis)
    place = lax.axis_index(axis)
    ahead = count - 1 - place if reverse else place
    gathered = jax.tree.map(lambda a: lax.all_gather(a, axis), part)
    state = jax.tree.map(lambda a, e: jnp.zeros_like(a) + jnp.asarray(e, a.dtype), part, identity)

    def one(hop, state):
        source = count - 1 - hop if reverse else hop
        return combine(
            state, jax.tree.map(lambda a: lax.dynamic_index_in_dim(a, source, 0, False), gathered)
        )

    return lax.fori_loop(0, ahead, one, state)


def group_pass(values, input_vectors, readout, step_sizes, decay_rates, skip_gain, initial):
    total_length, local_heads, head_width = values.shape
    block_count = total_length // GROUP
    state_width = input_vectors.shape[-1]
    value_blocks = values.reshape(block_count, GROUP, local_heads, head_width)
    input_blocks = input_vectors.reshape(block_count, GROUP, state_width)
    readout_blocks = readout.reshape(block_count, GROUP, state_width)
    step_blocks = step_sizes.reshape(block_count, GROUP, local_heads)
    row_index = lax.broadcasted_iota(jnp.int32, (GROUP, GROUP), 0)
    column_index = lax.broadcasted_iota(jnp.int32, (GROUP, GROUP), 1)
    causal = (row_index >= column_index)[:, :, None]

    def advance(carried_state, block_item):
        block_values, block_inputs, block_readout, block_steps = block_item
        cumulative = jnp.cumsum(block_steps * decay_rates[None, :], axis=0)
        log_gaps = jnp.where(causal, cumulative[:, None, :] - cumulative[None, :, :], 0.0)
        decay_weights = jnp.where(causal, jnp.exp(log_gaps), 0.0)
        scores = jnp.dot(block_readout, block_inputs.T, precision=highest)
        mixing = scores[:, :, None] * decay_weights * block_steps[None, :, :]
        within = jnp.einsum("tsh,shp->thp", mixing, block_values, precision=highest)
        carried = jnp.exp(cumulative)[:, :, None] * jnp.einsum(
            "tn,hpn->thp", block_readout, carried_state, precision=highest
        )
        outputs = within + carried + skip_gain[None, :, None] * block_values
        tail_weight = jnp.exp(cumulative[-1:, :] - cumulative) * block_steps
        next_state = jnp.exp(cumulative[-1])[:, None, None] * carried_state + jnp.einsum(
            "sh,sn,shp->hpn", tail_weight, block_inputs, block_values, precision=highest
        )
        return (next_state, (outputs, cumulative))

    final_state, (outputs, cumulatives) = lax.scan(
        advance, initial, (value_blocks, input_blocks, readout_blocks, step_blocks)
    )
    return (outputs.reshape(total_length, local_heads, head_width), final_state, cumulatives)


def mixer(values, input_vectors, readout, step_raw, step_bias, decay_log, skip_gain, initial):
    step_sizes = jax.nn.softplus(step_raw + step_bias[None, :])
    decay_rates = -jnp.exp(decay_log)
    outputs, final_state, cumulatives = group_pass(
        values, input_vectors, readout, step_sizes, decay_rates, skip_gain, initial
    )
    return (outputs, final_state)


def batched_mixer(
    values, input_vectors, readout, step_raw, step_bias, decay_log, skip_gain, initial
):
    return jax.vmap(mixer, in_axes=(0, 0, 0, 0, None, None, None, 0))(
        values, input_vectors, readout, step_raw, step_bias, decay_log, skip_gain, initial
    )


def silu_slope(inputs):
    sigmoid_values = jax.nn.sigmoid(inputs)
    return sigmoid_values * (1.0 + inputs * (1.0 - sigmoid_values))


def chain(earlier, later):
    return (earlier[0] * later[0], later[0][:, :, None, None] * earlier[1] + later[1])


def per_device(
    block_in,
    out_cotangent,
    norm_gain,
    gate_proj,
    value_proj,
    state_proj,
    step_proj,
    conv_value,
    conv_state,
    conv_value_bias,
    conv_state_bias,
    step_bias,
    decay_log,
    skip_gain,
    gated_gain,
    out_proj,
):
    sequences, block_length, model_width = block_in.shape
    token_rows = sequences * block_length
    local_heads = step_proj.shape[1]
    inner_width = gate_proj.shape[1]
    head_width = inner_width // local_heads
    state_part = state_proj.shape[2]
    conv_taps = conv_value.shape[0]
    channels = inner_width + 2 * state_part
    full_inner = inner_width * lax.axis_size("head")
    flat_in = block_in.reshape(token_rows, model_width).astype(jnp.float32)
    inv_rms = lax.rsqrt(jnp.mean(flat_in * flat_in, axis=1, keepdims=True) + 1e-05)
    normed = (flat_in * inv_rms * norm_gain[None, :]).astype(jnp.bfloat16)
    gate_pre = jnp.dot(normed, gate_proj, preferred_element_type=jnp.float32).astype(jnp.bfloat16)
    value_pre = jnp.dot(normed, value_proj, preferred_element_type=jnp.float32).astype(jnp.bfloat16)
    state_pre = jnp.einsum(
        "td,kdn->tkn", normed, state_proj, preferred_element_type=jnp.float32
    ).astype(jnp.bfloat16)
    step_raw = jnp.dot(normed, step_proj, preferred_element_type=jnp.float32).reshape(
        sequences, block_length, local_heads
    )
    conv_in = jnp.concatenate(
        [value_pre, state_pre.reshape(token_rows, 2 * state_part)], axis=1
    ).reshape(sequences, block_length, channels)
    conv_weight = jnp.concatenate(
        [conv_value, conv_state.reshape(conv_taps, 2 * state_part)], axis=1
    )
    conv_bias = jnp.concatenate([conv_value_bias, conv_state_bias.reshape(2 * state_part)])
    edge_rows = shifted(conv_in[:, block_length - (conv_taps - 1) :], "seq", 1)
    padded = jnp.concatenate([edge_rows, conv_in], axis=1).astype(jnp.float32)
    pre_act = jnp.zeros((sequences, block_length, channels), jnp.float32) + conv_bias[None, None, :]
    for tap_index in range(conv_taps):
        pre_act = (
            pre_act
            + conv_weight[tap_index][None, None, :]
            * padded[:, tap_index : tap_index + block_length]
        )
    activated = jax.nn.silu(pre_act).astype(jnp.bfloat16)
    values = (
        activated[:, :, :inner_width]
        .astype(jnp.float32)
        .reshape(sequences, block_length, local_heads, head_width)
    )
    state_local = activated[:, :, inner_width:].reshape(sequences, block_length, 2, state_part)
    state_full = lax.all_gather(state_local, "head", axis=3, tiled=True)
    input_vectors = state_full[:, :, 0].astype(jnp.float32)
    readout = state_full[:, :, 1].astype(jnp.float32)
    step_sizes = jax.nn.softplus(step_raw + step_bias[None, None, :])
    decay_rates = -jnp.exp(decay_log)
    zero_state = jnp.zeros((sequences, local_heads, head_width, readout.shape[-1]), jnp.float32)
    local_out, local_final, cumulatives = jax.vmap(group_pass, in_axes=(0, 0, 0, 0, None, None, 0))(
        values, input_vectors, readout, step_sizes, decay_rates, skip_gain, zero_state
    )
    block_totals = cumulatives[:, :, -1, :]
    offsets = jnp.cumsum(block_totals, axis=1) - block_totals
    through = (cumulatives + offsets[:, :, None, :]).reshape(sequences, block_length, local_heads)
    block_decay = jnp.exp(through[:, -1, :])
    identity = (jnp.ones_like(block_decay), jnp.zeros_like(local_final))
    unused_decay, incoming = entering((block_decay, local_final), "seq", chain, identity, False)
    carried = jnp.exp(through)[:, :, :, None] * jnp.einsum(
        "stn,shpn->sthp", readout, incoming, precision=highest
    )
    mixed = (local_out + carried).reshape(token_rows, inner_width)
    gate_value = gate_pre.astype(jnp.float32)
    gate_act = jax.nn.silu(gate_value)
    gated = mixed * gate_act
    total_squares = lax.psum(jnp.sum(gated * gated, axis=1), "head")
    gated_rms = lax.rsqrt(total_squares / full_inner + 1e-05)[:, None]
    gated_norm = (gated * gated_rms * gated_gain[None, :]).astype(jnp.bfloat16)
    share_rows = token_rows // lax.axis_size("head")
    branch_share = lax.psum_scatter(
        jnp.dot(gated_norm, out_proj, preferred_element_type=jnp.float32),
        "head",
        scatter_dimension=0,
        tiled=True,
    )
    own_start = lax.axis_index("head") * share_rows
    own_input = lax.dynamic_slice_in_dim(flat_in, own_start, share_rows, 0)
    out_piece = (own_input + branch_share).astype(jnp.bfloat16)
    block_out = lax.all_gather(out_piece, "head", axis=0, tiled=True).reshape(
        sequences, block_length, model_width
    )
    cotangent = out_cotangent.reshape(token_rows, model_width)
    d_norm_out = jnp.einsum("td,cd->tc", cotangent, out_proj, preferred_element_type=jnp.float32)
    out_proj_grad = jnp.einsum(
        "tc,td->cd", gated_norm, cotangent, preferred_element_type=jnp.float32
    )
    gated_gain_grad = jnp.sum(d_norm_out * gated * gated_rms, axis=0)
    scaled = d_norm_out * gated_gain[None, :]
    total_dot = lax.psum(jnp.sum(scaled * gated, axis=1), "head")
    d_gated = gated_rms * scaled - gated * gated_rms**3 * (total_dot / full_inner)[:, None]
    d_mixed = (d_gated * gate_act).reshape(sequences, block_length, local_heads, head_width)
    d_gate = (d_gated * mixed * silu_slope(gate_value)).astype(jnp.bfloat16)
    direct = jnp.einsum("sth,sthp,stn->shpn", jnp.exp(through), d_mixed, readout, precision=highest)
    unused_back, onward = entering((block_decay, direct), "seq", chain, identity, True)
    primal, pullback = jax.vjp(
        batched_mixer,
        values,
        input_vectors,
        readout,
        step_raw,
        step_bias,
        decay_log,
        skip_gain,
        incoming,
    )
    (
        d_values,
        d_inputs,
        d_readout,
        d_step_raw,
        step_bias_grad,
        decay_grad,
        skip_grad,
        unused_state,
    ) = pullback((d_mixed, onward))
    d_state = lax.psum_scatter(
        jnp.stack([d_inputs, d_readout], axis=2), "head", scatter_dimension=3, tiled=True
    )
    d_act = jnp.concatenate(
        [
            d_values.reshape(sequences, block_length, inner_width),
            d_state.reshape(sequences, block_length, 2 * state_part),
        ],
        axis=2,
    )
    d_pre = d_act * silu_slope(pre_act)
    next_rows = shifted(d_pre[:, : conv_taps - 1], "seq", -1)
    d_extended = jnp.concatenate([d_pre, next_rows], axis=1)
    d_conv_in = jnp.zeros_like(d_pre)
    conv_terms = []
    for tap_index in range(conv_taps):
        offset = conv_taps - 1 - tap_index
        d_conv_in = (
            d_conv_in
            + conv_weight[tap_index][None, None, :] * d_extended[:, offset : offset + block_length]
        )
        conv_terms.append(
            jnp.sum(d_pre * padded[:, tap_index : tap_index + block_length], axis=(0, 1))
        )
    conv_grad = jnp.stack(conv_terms)
    conv_bias_grad = jnp.sum(d_pre, axis=(0, 1))
    d_conv_flat = d_conv_in.reshape(token_rows, channels).astype(jnp.bfloat16)
    d_value_pre = d_conv_flat[:, :inner_width]
    d_state_pre = d_conv_flat[:, inner_width:].reshape(token_rows, 2, state_part)
    d_step = d_step_raw.reshape(token_rows, local_heads).astype(jnp.bfloat16)
    gate_grad = jnp.einsum("td,tc->dc", normed, d_gate, preferred_element_type=jnp.float32)
    value_grad = jnp.einsum("td,tc->dc", normed, d_value_pre, preferred_element_type=jnp.float32)
    state_grad = jnp.einsum("td,tkn->kdn", normed, d_state_pre, preferred_element_type=jnp.float32)
    step_grad = jnp.einsum("td,th->dh", normed, d_step, preferred_element_type=jnp.float32)
    partial_normed = jnp.einsum("tc,dc->td", d_gate, gate_proj, preferred_element_type=jnp.float32)
    partial_normed = partial_normed + jnp.einsum(
        "tc,dc->td", d_value_pre, value_proj, preferred_element_type=jnp.float32
    )
    partial_normed = partial_normed + jnp.einsum(
        "tkn,kdn->td", d_state_pre, state_proj, preferred_element_type=jnp.float32
    )
    partial_normed = partial_normed + jnp.einsum(
        "th,dh->td", d_step, step_proj, preferred_element_type=jnp.float32
    )
    d_normed = lax.psum(partial_normed, "head")
    norm_grad = jnp.sum(d_normed * flat_in * inv_rms, axis=0)
    scaled_in = d_normed * norm_gain[None, :]
    input_grad = (
        cotangent.astype(jnp.float32)
        + inv_rms * scaled_in
        - flat_in * inv_rms**3 * jnp.mean(scaled_in * flat_in, axis=1, keepdims=True)
    )
    conv_value_grad = conv_grad[:, :inner_width]
    conv_state_grad = conv_grad[:, inner_width:].reshape(conv_taps, 2, state_part)
    conv_value_bias_grad = conv_bias_grad[:inner_width]
    conv_state_bias_grad = conv_bias_grad[inner_width:].reshape(2, state_part)
    summed = tuple(
        lax.psum(
            (
                norm_grad,
                gate_grad,
                value_grad,
                state_grad,
                step_grad,
                conv_value_grad,
                conv_state_grad,
                conv_value_bias_grad,
                conv_state_bias_grad,
                step_bias_grad,
                decay_grad,
                skip_grad,
                gated_gain_grad,
                out_proj_grad,
            ),
            ("seq", "sample"),
        )
    )
    return (block_out, input_grad.reshape(sequences, block_length, model_width)) + summed


def solution(mesh):
    return jax.shard_map(
        per_device,
        mesh=mesh,
        in_specs=(
            P("sample", "seq", None),
            P("sample", "seq", None),
            P(),
            P(None, "head"),
            P(None, "head"),
            P(None, None, "head"),
            P(None, "head"),
            P(None, "head"),
            P(None, None, "head"),
            P("head"),
            P(None, "head"),
            P("head"),
            P("head"),
            P("head"),
            P("head"),
            P("head", None),
        ),
        out_specs=(
            P("sample", "seq", None),
            P("sample", "seq", None),
            P(),
            P(None, "head"),
            P(None, "head"),
            P(None, None, "head"),
            P(None, "head"),
            P(None, "head"),
            P(None, None, "head"),
            P("head"),
            P(None, "head"),
            P("head"),
            P("head"),
            P("head"),
            P("head"),
            P("head", None),
        ),
        check_vma=False,
    )
```

profile of v0, /device:TPU:0, one launch (start us, length us, event | category | flops | bytes accessed | tf_op | source)
XLA Modules:
  0.0 856.5 jit_solution(13407658360489493288)
XLA Ops:
  19.7 5.6 collective-permute-start
  36.5 15.6 %all_gather.24 = bf16[2,512,2,128]{1,2,0,3:T(2,128)(2,1)S(1)} all-gather(bf16[2,512,2,32]{1,2,0,3:T(2,128)(2,1)S(1)} %copy.200), channel_id=1, replica_groups=mesh['seq'=4,'sample'=2,'head'=4] {'head'}, dimensions={3}, use_global_device_ids=true | all-gather | bytes 655360 | tf_op jit(solution)/shard_map/all_gather | solution.py:155
  68.6 29.9 %while.120 = (s32[]{:T(128)}, f32[2,8,64,128]{3,2,1,0:T(8,128)}, f32[2,2,256,8,64]{2,4,3,1,0:T(8,128)}, f32[2,2,256,8]{2,3,1,0:T(8,128)S(1)}, f32[2,2,256,8]{2,3...) while((s32[]{:T(128)}, f32[2,8,64,128]{3,2,1,0:T(8,128)}, ...), condition=%wide.region_4.5_spmd.clone.clone, body=%wide.region_1.4_spmd.clone.clone.sunk | while | flops 1819623424 | bytes 16686640 | solution.py:62
  71.7 5.9 fusion.268
  86.6 5.9 fusion.268
  104.1 10.1 %all-gather = f32[8,1,8]{2,1,0:T(1,128)S(1)} all-gather(f32[2,1,8]{2,1,0:T(1,128)S(1)} %slice_exponential_fusion), channel_id=2, replica_groups=mesh['seq'=4,'sample'=2,'head'=4] {'seq'}, dimensions={0}, use_global_device_ids=true | all-gather | bytes 320 | tf_op jit(solution)/shard_map/all_gather | solution.py:20
  121.1 15.5 %all-gather.9.cloned.1.call-done = f32[8,8,64,128]{3,2,1,0:T(8,128)} async-done(((f32[2,8,64,128]{3,2,1,0:T(8,128)}), f32[8,8,64,128]{3,2,1,0:T(8,128)}) %all-gather.9.cloned.1.call-update) | async-done | bytes 2097168 | tf_op jit(solution)/shard_map/all_gather | solution.py:20
  147.2 11.7 %psum.119 = f32[1024]{0:T(1024)S(1)} all-reduce(f32[1024]{0:T(1024)S(1)} %get-tuple-element.2065), channel_id=1, replica_groups=mesh['seq'=4,'sample'=2,'head'=4] {'head'}, use_global_device_ids=true, to_apply=%region_9.10 | all-reduce | flops 1024 | bytes 8192 | tf_op jit(solution)/shard_map/psum | solution.py:177
  158.9 6.2 multiply_reduce_fusion.7
  165.1 8.3 psum.120
  173.4 5.6 fusion.149
  191.7 43.1 %while.119 = (s32[]{:T(128)}, f32[2,8,64,128]{3,2,1,0:T(8,128)}, f32[2,2,256,256,8]{3,4,2,1,0:T(8,128)}, f32[2,2,128,256]{2,3,1,0:T(8,128)}, f32[2,2,256,256,8]{...) while((s32[]{:T(128)}, f32[2,8,64,128]{3,2,1,0:T(8,128)}, ...), condition=%wide.region_18.19_spmd.clone.clone, body=%wide.region_15.18_spmd.clone.clone.sunk | while | flops 1013198912 | bytes 70188120 | solution.py:62
  196.4 6.8 multiply_dynamic-update-slice_fusion.2
  218.1 6.6 multiply_dynamic-update-slice_fusion.2
  243.0 6.3 while.118
  253.5 137.8 %while.121 = (s32[]{:T(128)}, f32[8]{0:T(128)}, f32[8]{0:T(128)}, f32[2,8,64,128]{3,2,1,0:T(8,128)}, f32[2,2,256,8,64]{2,4,3,1,0:T(8,128)}, /*index=5*/f32[2,2,2...) while((s32[]{:T(128)}, f32[8]{0:T(128)}, f32[8]{0:T(128)}, ...), condition=%wide.region_31.32_spmd.clone.clone, body=%wide.region_19.31_spmd.clone.clone.sunk | while | flops 3639656448 | bytes 113358104 | solution.py:62
  253.9 6.0 constant_dynamic-slice_fusion.13
  264.9 10.5 %fusion.281 = (f32[2,256,8]{1,2,0:T(8,128)S(1)}, f32[2,256,8]{1,2,0:T(8,128)S(1)}, f32[2,256,256]{2,1,0:T(8,128)}, f32[2,256,8]{1,2,0:T(8,128)S(1)}) fusion(f32[1,2,256,256,8]{3,4,2,1,0:T(8,128)S(1)} %get-tuple-element.2591, f32[2,256,8]{1,2,0:T(8,128)S(1)} %dynamic-slice_bitcast_fusion.18, f32[2,256,256]{2,1,0:T(8,128)S(1)} %dynamic-slice_bitcast_fusion.19, ...), kind=kOutput, calls=%fused_computation.155.clone.1 | convolution fusion | flops 816697344 | bytes 15860736 | tf_op jit(solution)/shard_map/transpose(jvp(vmap()))/while/body/eval_jaxpr/tsh,shp->thp/dot_general | solution.py:51
  292.7 5.0 reduce-window.68
  322.6 6.0 constant_dynamic-slice_fusion.13
  333.6 10.5 %fusion.281 = (f32[2,256,8]{1,2,0:T(8,128)S(1)}, f32[2,256,8]{1,2,0:T(8,128)S(1)}, f32[2,256,256]{2,1,0:T(8,128)}, f32[2,256,8]{1,2,0:T(8,128)S(1)}) fusion(f32[1,2,256,256,8]{3,4,2,1,0:T(8,128)S(1)} %get-tuple-element.2591, f32[2,256,8]{1,2,0:T(8,128)S(1)} %dynamic-slice_bitcast_fusion.18, f32[2,256,256]{2,1,0:T(8,128)S(1)} %dynamic-slice_bitcast_fusion.19, ...), kind=kOutput, calls=%fused_computation.155.clone.1 | convolution fusion | flops 816697344 | bytes 15860736 | tf_op jit(solution)/shard_map/transpose(jvp(vmap()))/while/body/eval_jaxpr/tsh,shp->thp/dot_general | solution.py:51
  361.3 5.0 reduce-window.68
  382.9 4.9 fusion.290
  402.9 5.0 fusion.180
  415.0 31.8 %all-reduce.11.cloned.1.call-done = f32[2,512,2,128]{1,2,0,3:T(2,128)} async-done(((f32[2,512,2,128]{1,2,0,3:T(2,128)}), f32[2,512,2,128]{1,2,0,3:T(2,128)}) %all-reduce.11.cloned.1.call-update) | async-done | bytes 1048592
  447.9 8.2 multiply_reduce_fusion.6
  463.7 6.2 fusion.151
  481.2 44.4 %reduce-scatter.2.cloned.1.call-done = f32[256,1024]{1,0:T(8,128)} async-done(((f32[1024,1024]{1,0:T(8,128)}), f32[256,1024]{1,0:T(8,128)}) %reduce-scatter.2.cloned.1.call-update) | async-done | bytes 1048592 | tf_op jit(solution)/shard_map/reduce_scatter | solution.py:181
  543.0 140.4 %all-reduce.9.cloned.1.call-done = f32[1024,1024]{1,0:T(8,128)} async-done(((f32[1024,1024]{1,0:T(8,128)}), f32[1024,1024]{1,0:T(8,128)}) %all-reduce.9.cloned.1.call-update) | async-done | bytes 4194320 | tf_op jit(solution)/shard_map/psum | solution.py:271
  686.9 26.1 %all-reduce.3 = (f32[1024]{0:T(1024)}, f32[1024,8]{0,1:T(8,128)}, f32[4,512]{1,0:T(4,128)}, f32[4,2,32]{2,1,0:T(2,128)}, f32[512]{0:T(512)}, /*index=5*/f32[2,32...) all-reduce(f32[1024]{0:T(1024)S(1)} %get-tuple-element.1844, ...), channel_id=1, replica_groups=mesh['seq'=4,'sample'=2,'head'=4] {'seq','sample'}, use_global_device_ids=true, to_apply=%region_36.37 | all-reduce | flops 12632 | bytes 101056 | tf_op jit(solution)/shard_map/psum | solution.py:284
  717.8 11.6 %all-gather.7.cloned.1.call-done = bf16[1024,1024]{1,0:T(8,128)(2,1)} async-done(((bf16[256,1024]{1,0:T(8,128)(2,1)}), bf16[1024,1024]{1,0:T(8,128)(2,1)}) %all-gather.7.cloned.1.call-update) | async-done | bytes 2097168 | tf_op jit(solution)/shard_map/all_gather | solution.py:190
  729.4 110.5 %all-reduce.13.cloned.1.call-done = (f32[1024,512]{1,0:T(8,128)}, f32[1024,512]{1,0:T(8,128)}, f32[2,1024,32]{1,2,0:T(8,128)}, f32[512,1024]{1,0:T(8,128)}) async-done(((f32[1024,512]{1,0:T(8,128)}, f32[1024,512]{1,0:T(8,128)}, f32[2,1024,32]{1,2,0:T(8,128)}, f32[512,1024]{1,0:T(8,128)}), (f32[1024,512]{1,0:T(8,128)}, f32[1024,512]{1,0:T(8,128)}, f32[2,1024,32]{1,2,0:T(8,128)}, ...) | async-done | bytes 6553616 | tf_op jit(solution)/shard_map/psum | solution.py:284
  (582 shorter events, 303.0 us)
Async XLA Ops:
  7.2 151.7 %copy-start = (bf16[512,1024]{1,0:T(8,128)(2,1)S(1)}, bf16[512,1024]{1,0:T(8,128)(2,1)}, u32[]{:S(2)}) copy-start(bf16[512,1024]{1,0:T(8,128)(2,1)} %param.41) | copy-start | bytes 3145732
  7.2 129.4 %all-gather.9.cloned.1.call-start = ((), (), s32[]{:S(2)}) async-start(), calls=%async_computation.4 | async-start | bytes 2621440 | tf_op jit(solution)/shard_map/all_gather | solution.py:20
  15.3 9.9 %copy-start.90 = (f32[4,512]{1,0:T(4,128)S(1)}, f32[4,512]{1,0:T(4,128)}, u32[]{:S(2)}) copy-start(f32[4,512]{1,0:T(4,128)} %param.33) | copy-start | bytes 24580
  15.3 9.9 %copy-start.91 = (f32[4,2,32]{2,1,0:T(2,128)S(1)}, f32[4,2,32]{2,1,0:T(2,128)}, u32[]{:S(2)}) copy-start(f32[4,2,32]{2,1,0:T(2,128)} %param.34) | copy-start | bytes 3076
  15.3 10.1 %copy-start.100 = (f32[2,32]{1,0:T(2,128)S(1)}, f32[2,32]{1,0:T(2,128)}, u32[]{:S(2)}) copy-start(f32[2,32]{1,0:T(2,128)} %param.36) | copy-start | bytes 772
  19.7 11.4 %collective-permute-start = (bf16[2,3,576]{1,2,0:T(8,128)(2,1)}, bf16[2,3,576]{1,2,0:T(8,128)(2,1)}, u32[]{:S(2)}, u32[]{:S(2)}) collective-permute-start(bf16[2,3,576]{1,2,0:T(8,128)(2,1)} %pad_maximum_fusion.2), channel_id=1, source_target_pairs={{0,8},{8,16},{16,24},{1,9},{9,17},{17,25},{2,10},{10,18},{18,26},{... | collective-permute-start | bytes 20744 | tf_op jit(solution)/shard_map/ppermute | solution.py:13
  98.5 143.7 %all-gather.11.cloned.1.call-start = ((), (), s32[]{:S(2)}) async-start(), calls=%async_computation.5 | async-start | bytes 2621440 | tf_op jit(solution)/shard_map/all_gather | solution.py:20
  144.6 14.3 %copy-start.92 = (f32[512]{0:T(512)S(1)}, f32[512]{0:T(512)}, u32[]{:S(2)}) copy-start(f32[512]{0:T(512)} %param.40) | copy-start | bytes 6148
  158.9 14.5 %copy-start.79 = (f32[1024]{0:T(1024)}, f32[1024]{0:T(1024)S(1)}, u32[]{:S(2)}) copy-start(f32[1024]{0:T(1024)S(1)} %get-tuple-element.2058) | copy-start | bytes 12292
  186.7 260.1 %all-reduce.11.cloned.1.call-start = ((), (), s32[]{:S(2)}) async-start(), calls=%async_computation.6 | async-start | bytes 2097152
  203.7 8.2 copy-start.19
  225.1 8.3 copy-start.19
  287.5 15.4 %copy-start.87 = (f32[8]{0:T(128)S(1)}, f32[8]{0:T(128)}, u32[]{:S(2)}) copy-start(f32[8]{0:T(128)} %get-tuple-element.2809) | copy-start | bytes 100 | tf_op jit(solution)/shard_map/transpose(jvp(vmap()))/while
  302.9 9.5 %copy-start.88 = (f32[8]{0:T(128)}, f32[8]{0:T(128)S(1)}, u32[]{:S(2)}) copy-start(f32[8]{0:T(128)S(1)} %fusion.287) | copy-start | bytes 100 | tf_op jit(solution)/shard_map/transpose(jvp(vmap()))/while
  303.7 8.7 %copy-start.8 = (f32[2,2,256,128]{3,2,1,0:T(8,128)S(1)}, f32[2,2,256,128]{3,2,1,0:T(8,128)}, u32[]{:S(2)}) copy-start(f32[2,2,256,128]{3,2,1,0:T(8,128)} %get-tuple-element.2865) | copy-start | bytes 1572868 | tf_op jit(solution)/shard_map/transpose(jvp(vmap()))/while
  303.7 10.5 %copy-start.9 = (f32[2,256,8,64]{1,3,2,0:T(8,128)S(1)}, f32[2,256,8,64]{1,3,2,0:T(8,128)}, u32[]{:S(2)}) copy-start(f32[2,256,8,64]{1,3,2,0:T(8,128)} %get-tuple-element.2602) | copy-start | bytes 3145732 | tf_op jit(solution)/shard_map/transpose(jvp(vmap()))/while
  356.2 15.4 %copy-start.87 = (f32[8]{0:T(128)S(1)}, f32[8]{0:T(128)}, u32[]{:S(2)}) copy-start(f32[8]{0:T(128)} %get-tuple-element.2809) | copy-start | bytes 100 | tf_op jit(solution)/shard_map/transpose(jvp(vmap()))/while
  371.6 9.5 %copy-start.88 = (f32[8]{0:T(128)}, f32[8]{0:T(128)S(1)}, u32[]{:S(2)}) copy-start(f32[8]{0:T(128)S(1)} %fusion.287) | copy-start | bytes 100 | tf_op jit(solution)/shard_map/transpose(jvp(vmap()))/while
  372.4 8.7 %copy-start.8 = (f32[2,2,256,128]{3,2,1,0:T(8,128)S(1)}, f32[2,2,256,128]{3,2,1,0:T(8,128)}, u32[]{:S(2)}) copy-start(f32[2,2,256,128]{3,2,1,0:T(8,128)} %get-tuple-element.2865) | copy-start | bytes 1572868 | tf_op jit(solution)/shard_map/transpose(jvp(vmap()))/while
  372.4 10.5 %copy-start.9 = (f32[2,256,8,64]{1,3,2,0:T(8,128)S(1)}, f32[2,256,8,64]{1,3,2,0:T(8,128)}, u32[]{:S(2)}) copy-start(f32[2,256,8,64]{1,3,2,0:T(8,128)} %get-tuple-element.2602) | copy-start | bytes 3145732 | tf_op jit(solution)/shard_map/transpose(jvp(vmap()))/while
  396.1 129.5 %reduce-scatter.2.cloned.1.call-start = ((), (), s32[]{:S(2)}) async-start(), calls=%async_computation.1 | async-start | bytes 5242880 | tf_op jit(solution)/shard_map/reduce_scatter | solution.py:181
  401.0 282.3 %all-reduce.9.cloned.1.call-start = ((), (), s32[]{:S(2)}) async-start(), calls=%async_computation.3 | async-start | bytes 8388608 | tf_op jit(solution)/shard_map/psum | solution.py:271
  456.1 7.6 copy-start.69
  456.1 7.6 copy-start.71
  456.1 7.6 copy-start.73
  456.1 7.6 copy-start.75
  457.8 5.6 collective-permute-start.1
  477.0 252.4 %all-gather.7.cloned.1.call-start = ((), (), s32[]{:S(2)}) async-start(), calls=%async_computation.2 | async-start | bytes 2621440 | tf_op jit(solution)/shard_map/all_gather | solution.py:190
  528.1 311.9 %all-reduce.13.cloned.1.call-start = ((), (), s32[]{:S(2)}) async-start(), calls=%async_computation.7 | async-start | bytes 13107200 | tf_op jit(solution)/shard_map/psum | solution.py:284
  540.7 142.7 %copy-start.64 = (f32[1024]{0:T(1024)S(1)}, f32[1024]{0:T(1024)}, u32[]{:S(2)}) copy-start(f32[1024]{0:T(1024)} %param.28) | copy-start | bytes 12292
  543.0 143.9 %copy-start.78 = (f32[8]{0:T(128)S(1)}, f32[8]{0:T(128)}, u32[]{:S(2)}) copy-start(f32[8]{0:T(128)} %get-tuple-element.1204) | copy-start | bytes 100
  543.0 143.9 %copy-start.94 = (f32[512]{0:T(512)S(1)}, f32[512]{0:T(512)}, u32[]{:S(2)}) copy-start(f32[512]{0:T(512)} %get-tuple-element.1850) | copy-start | bytes 6148
  (122 other events, 462.1 us)
Sparse Core Ops, SparseCore 0:
  98.6 37.9 all-gather.8
  186.8 40.2 all-gather.10
  396.2 50.5 all-reduce.10
  449.5 76.0 reduce-scatter.1
  527.8 155.5 all-reduce.8
  684.8 44.6 all-gather.6
  734.2 105.6 all-reduce.12
where the time goes:
time: 865 us; the launch traced here: 856 us
  waiting for transfers between devices  360 us (42%)
  matrix products  155 us (18%)
  local copies, waits for them, and re-layouts  138 us (16%)
  other arithmetic  107 us (12%)
  blocking collectives  71.8 us (8%)
  between operations  15.9 us (2%)
    psum x1, waiting for transfers between devices, per_device(): d_normed = lax.psum(partial_normed, 'head')  140 us
    psum x1, waiting for transfers between devices, per_device(): lax.psum((norm_grad, gate_grad, value_grad, state_grad, step_grad, conv_v...  111 us
    reduce_scatter x1, waiting for transfers between devices, per_device(): lax.psum_scatter(jnp.dot(gated_norm, out_proj, preferred_element_type=jnp...  44.4 us
    dot_general x6, matrix products, advance(): within = jnp.einsum('tsh,shp->thp', mixing, block_values, precision=highest)  42.7 us
    unnamed x8, waiting for transfers between devices  31.9 us
    unnamed x139, local copies, waits for them, and re-layouts  27.6 us
    psum x1, blocking collectives, per_device(): lax.psum((norm_grad, gate_grad, value_grad, state_grad, step_grad, conv_v...  26.1 us
    dynamic_slice x10, local copies, waits for them, and re-layouts, group_pass(): lax.scan(advance, initial, (value_blocks, input_blocks, readout_blocks, s...  25.2 us
  transfers between devices with their start and end apart: 9, of which 8 were waited for; matrix products, arithmetic and copies ran while one was open for 15% of the time, Pallas kernels for 0%

commit v1 on v0

--- a/solution.py
+++ b/solution.py
@@ -282,23 +282,26 @@
     conv_state_bias_grad = conv_bias_grad[inner_width:].reshape(2, state_part)
     summed = tuple(
         lax.psum(
-            (
-                norm_grad,
-                gate_grad,
-                value_grad,
-                state_grad,
-                step_grad,
-                conv_value_grad,
-                conv_state_grad,
-                conv_value_bias_grad,
-                conv_state_bias_grad,
-                step_bias_grad,
-                decay_grad,
-                skip_grad,
-                gated_gain_grad,
-                out_proj_grad,
+            lax.psum(
+                (
+                    norm_grad,
+                    gate_grad,
+                    value_grad,
+                    state_grad,
+                    step_grad,
+                    conv_value_grad,
+                    conv_state_grad,
+                    conv_value_bias_grad,
+                    conv_state_bias_grad,
+                    step_bias_grad,
+                    decay_grad,
+                    skip_grad,
+                    gated_gain_grad,
+                    out_proj_grad,
+                ),
+                "sample",
             ),
-            ("seq", "sample"),
+            "seq",
         )
     )
     return (block_out, input_grad.reshape(sequences, block_length, model_width)) + summed

time: 865 us -> 938 us (1.084)
  waiting for transfers between devices: 360 us -> 439 us
    psum x0 -> x1, waiting for transfers between devices: none -> 145 us  [per_device(): lax.psum(lax.psum((norm_grad, gate_grad, value_grad, state_grad, step_gra...]
    psum x1, waiting for transfers between devices: 111 us -> 34.7 us  [per_device(): lax.psum((norm_grad, gate_grad, value_grad, state_grad, step_grad, conv_v...]
    psum x1, blocking collectives: 26.1 us -> 3.59 us  [per_device(): lax.psum((norm_grad, gate_grad, value_grad, state_grad, step_grad, conv_v...]
    psum x0 -> x1, blocking collectives: none -> 17.5 us  [per_device(): lax.psum(lax.psum((norm_grad, gate_grad, value_grad, state_grad, step_gra...]
    psum x1, waiting for transfers between devices: 140 us -> 155 us  [per_device(): d_normed = lax.psum(partial_normed, 'head')]
    reduce_scatter x1, waiting for transfers between devices: 44.4 us -> 33.7 us  [per_device(): lax.psum_scatter(jnp.dot(gated_norm, out_proj, preferred_element_type=jnp...]
    unnamed x8 -> x9, waiting for transfers between devices: 31.9 us -> 34.8 us
    unnamed x139 -> x129, local copies, waits for them, and re-layouts: 27.6 us -> 27.2 us
  transfers between devices with their start and end apart: 9 -> 10, of which waited for: 8 -> 8; matrix products, arithmetic and copies ran while one was open for 15% -> 14% of each run, Pallas kernels for 0% -> 0%
where the time goes in v1:
time: 938 us; the launch traced here: 930 us
  waiting for transfers between devices  439 us (47%)
  matrix products  157 us (17%)
  local copies, waits for them, and re-layouts  137 us (15%)
  other arithmetic  106 us (11%)
  blocking collectives  66.8 us (7%)
  between operations  15.9 us (2%)
    psum x1, waiting for transfers between devices, per_device(): d_normed = lax.psum(partial_normed, 'head')  155 us
    psum x1, waiting for transfers between devices, per_device(): lax.psum(lax.psum((norm_grad, gate_grad, value_grad, state_grad, step_gra...  145 us
    dot_general x6, matrix products, advance(): within = jnp.einsum('tsh,shp->thp', mixing, block_values, precision=highest)  42.8 us
    unnamed x9, waiting for transfers between devices  34.8 us
    psum x1, waiting for transfers between devices, per_device(): lax.psum((norm_grad, gate_grad, value_grad, state_grad, step_grad, conv_v...  34.7 us
    reduce_scatter x1, waiting for transfers between devices, per_device(): lax.psum_scatter(jnp.dot(gated_norm, out_proj, preferred_element_type=jnp...  33.7 us
    unnamed x129, local copies, waits for them, and re-layouts  27.2 us
    dynamic_slice x10, local copies, waits for them, and re-layouts, group_pass(): lax.scan(advance, initial, (value_blocks, input_blocks, readout_blocks, s...  25.2 us
  transfers between devices with their start and end apart: 10, of which 8 were waited for; matrix products, arithmetic and copies ran while one was open for 14% of the time, Pallas kernels for 0%

profile of v1, /device:TPU:0, one launch (start us, length us, event | category | flops | bytes accessed | tf_op | source)
XLA Modules:
  0.0 930.2 jit_solution(11560503058521303009)
XLA Ops:
  19.7 5.6 collective-permute-start
  36.5 15.6 %all_gather.24 = bf16[2,512,2,128]{1,2,0,3:T(2,128)(2,1)S(1)} all-gather(bf16[2,512,2,32]{1,2,0,3:T(2,128)(2,1)S(1)} %copy.200), channel_id=1, replica_groups=mesh['seq'=4,'sample'=2,'head'=4] {'head'}, dimensions={3}, use_global_device_ids=true | all-gather | bytes 655360 | tf_op jit(solution)/shard_map/all_gather | solution.py:155
  68.6 29.9 %while.120 = (s32[]{:T(128)}, f32[2,8,64,128]{3,2,1,0:T(8,128)}, f32[2,2,256,8,64]{2,4,3,1,0:T(8,128)}, f32[2,2,256,8]{2,3,1,0:T(8,128)S(1)}, f32[2,2,256,8]{2,3...) while((s32[]{:T(128)}, f32[2,8,64,128]{3,2,1,0:T(8,128)}, ...), condition=%wide.region_4.5_spmd.clone.clone, body=%wide.region_1.4_spmd.clone.clone.sunk | while | flops 1819623424 | bytes 16686640 | solution.py:62
  71.7 5.9 fusion.268
  86.6 5.9 fusion.268
  104.0 10.1 %all-gather = f32[8,1,8]{2,1,0:T(1,128)S(1)} all-gather(f32[2,1,8]{2,1,0:T(1,128)S(1)} %slice_exponential_fusion), channel_id=2, replica_groups=mesh['seq'=4,'sample'=2,'head'=4] {'seq'}, dimensions={0}, use_global_device_ids=true | all-gather | bytes 320 | tf_op jit(solution)/shard_map/all_gather | solution.py:20
  121.1 15.5 %all-gather.9.cloned.1.call-done = f32[8,8,64,128]{3,2,1,0:T(8,128)} async-done(((f32[2,8,64,128]{3,2,1,0:T(8,128)}), f32[8,8,64,128]{3,2,1,0:T(8,128)}) %all-gather.9.cloned.1.call-update) | async-done | bytes 2097168 | tf_op jit(solution)/shard_map/all_gather | solution.py:20
  147.2 11.7 %psum.217 = f32[1024]{0:T(1024)S(1)} all-reduce(f32[1024]{0:T(1024)S(1)} %get-tuple-element.2079), channel_id=1, replica_groups=mesh['seq'=4,'sample'=2,'head'=4] {'head'}, use_global_device_ids=true, to_apply=%region_9.10 | all-reduce | flops 1024 | bytes 8192 | tf_op jit(solution)/shard_map/psum | solution.py:177
  158.9 6.2 multiply_reduce_fusion.7
  165.1 8.3 psum.218
  173.4 5.6 fusion.149
  191.8 43.2 %while.119 = (s32[]{:T(128)}, f32[2,8,64,128]{3,2,1,0:T(8,128)}, f32[2,2,256,256,8]{3,4,2,1,0:T(8,128)}, f32[2,2,128,256]{2,3,1,0:T(8,128)}, f32[2,2,256,256,8]{...) while((s32[]{:T(128)}, f32[2,8,64,128]{3,2,1,0:T(8,128)}, ...), condition=%wide.region_18.19_spmd.clone.clone, body=%wide.region_15.18_spmd.clone.clone.sunk | while | flops 1013198912 | bytes 70188120 | solution.py:62
  196.5 6.8 multiply_dynamic-update-slice_fusion.2
  218.2 6.6 multiply_dynamic-update-slice_fusion.2
  243.2 6.3 while.118
  253.7 138.0 %while.121 = (s32[]{:T(128)}, f32[8]{0:T(128)}, f32[8]{0:T(128)}, f32[2,8,64,128]{3,2,1,0:T(8,128)}, f32[2,2,256,8,64]{2,4,3,1,0:T(8,128)}, /*index=5*/f32[2,2,2...) while((s32[]{:T(128)}, f32[8]{0:T(128)}, f32[8]{0:T(128)}, ...), condition=%wide.region_31.32_spmd.clone.clone, body=%wide.region_19.31_spmd.clone.clone.sunk | while | flops 3639656448 | bytes 113358104 | solution.py:62
  254.2 6.0 constant_dynamic-slice_fusion.13
  265.2 10.5 %fusion.281 = (f32[2,256,8]{1,2,0:T(8,128)S(1)}, f32[2,256,8]{1,2,0:T(8,128)S(1)}, f32[2,256,256]{2,1,0:T(8,128)}, f32[2,256,8]{1,2,0:T(8,128)S(1)}) fusion(f32[1,2,256,256,8]{3,4,2,1,0:T(8,128)S(1)} %get-tuple-element.2605, f32[2,256,8]{1,2,0:T(8,128)S(1)} %dynamic-slice_bitcast_fusion.18, f32[2,256,256]{2,1,0:T(8,128)S(1)} %dynamic-slice_bitcast_fusion.19, ...), kind=kOutput, calls=%fused_computation.155.clone.1 | convolution fusion | flops 816697344 | bytes 15860736 | tf_op jit(solution)/shard_map/transpose(jvp(vmap()))/while/body/eval_jaxpr/tsh,shp->thp/dot_general | solution.py:51
  292.9 5.0 reduce-window.68
  314.5 4.9 fusion.290
  322.9 6.0 constant_dynamic-slice_fusion.13
  333.9 10.5 %fusion.281 = (f32[2,256,8]{1,2,0:T(8,128)S(1)}, f32[2,256,8]{1,2,0:T(8,128)S(1)}, f32[2,256,256]{2,1,0:T(8,128)}, f32[2,256,8]{1,2,0:T(8,128)S(1)}) fusion(f32[1,2,256,256,8]{3,4,2,1,0:T(8,128)S(1)} %get-tuple-element.2605, f32[2,256,8]{1,2,0:T(8,128)S(1)} %dynamic-slice_bitcast_fusion.18, f32[2,256,256]{2,1,0:T(8,128)S(1)} %dynamic-slice_bitcast_fusion.19, ...), kind=kOutput, calls=%fused_computation.155.clone.1 | convolution fusion | flops 816697344 | bytes 15860736 | tf_op jit(solution)/shard_map/transpose(jvp(vmap()))/while/body/eval_jaxpr/tsh,shp->thp/dot_general | solution.py:51
  361.7 5.0 reduce-window.68
  412.5 34.7 %all-reduce.14.cloned.1.call-done = f32[2,512,2,128]{1,2,0,3:T(2,128)} async-done(((f32[2,512,2,128]{1,2,0,3:T(2,128)}), f32[2,512,2,128]{1,2,0,3:T(2,128)}) %all-reduce.14.cloned.1.call-update) | async-done | bytes 1048592
  448.3 8.3 multiply_reduce_fusion.6
  465.7 4.9 fusion.151
  492.4 33.7 %reduce-scatter.2.cloned.1.call-done = f32[256,1024]{1,0:T(8,128)} async-done(((f32[1024,1024]{1,0:T(8,128)}), f32[256,1024]{1,0:T(8,128)}) %reduce-scatter.2.cloned.1.call-update) | async-done | bytes 1048592 | tf_op jit(solution)/shard_map/reduce_scatter | solution.py:181
  528.6 34.7 %all-reduce.18.cloned.1.call-done = (f32[1024,512]{1,0:T(8,128)}, f32[1024,512]{1,0:T(8,128)}, f32[2,1024,32]{1,2,0:T(8,128)}, f32[512,1024]{1,0:T(8,128)}) async-done(((f32[1024,512]{1,0:T(8,128)}, f32[1024,512]{1,0:T(8,128)}, f32[2,1024,32]{1,2,0:T(8,128)}, f32[512,1024]{1,0:T(8,128)}), (f32[1024,512]{1,0:T(8,128)}, f32[1024,512]{1,0:T(8,128)}, f32[2,1024,32]{1,2,0:T(8,128)}, ...) | async-done | bytes 6553616 | tf_op jit(solution)/shard_map/psum | solution.py:285
  566.3 155.4 %all-reduce.12.cloned.1.call-done = f32[1024,1024]{1,0:T(8,128)} async-done(((f32[1024,1024]{1,0:T(8,128)}), f32[1024,1024]{1,0:T(8,128)}) %all-reduce.12.cloned.1.call-update) | async-done | bytes 4194320 | tf_op jit(solution)/shard_map/psum | solution.py:271
  728.9 17.5 %all-reduce.3 = (f32[1024]{0:T(1024)}, f32[1024,8]{0,1:T(8,128)}, f32[4,512]{1,0:T(4,128)}, f32[4,2,32]{2,1,0:T(2,128)}, f32[512]{0:T(512)}, /*index=5*/f32[2,32...) all-reduce(f32[1024]{0:T(1024)S(1)} %get-tuple-element.2023, ...), channel_id=1, replica_groups=mesh['seq'=4,'sample'=2,'head'=4] {'seq'}, use_global_device_ids=true, to_apply=%region_37.38 | all-reduce | flops 12632 | bytes 101056 | tf_op jit(solution)/shard_map/psum | solution.py:284
  751.1 17.4 %all-gather.7.cloned.1.call-done = bf16[1024,1024]{1,0:T(8,128)(2,1)} async-done(((bf16[256,1024]{1,0:T(8,128)(2,1)}), bf16[1024,1024]{1,0:T(8,128)(2,1)}) %all-gather.7.cloned.1.call-update) | async-done | bytes 2097168 | tf_op jit(solution)/shard_map/all_gather | solution.py:190
  768.5 145.2 %all-reduce.16.cloned.1.call-done = (f32[1024,512]{1,0:T(8,128)}, f32[1024,512]{1,0:T(8,128)}, f32[2,1024,32]{1,2,0:T(8,128)}, f32[512,1024]{1,0:T(8,128)}) async-done(((f32[1024,512]{1,0:T(8,128)}, f32[1024,512]{1,0:T(8,128)}, f32[2,1024,32]{1,2,0:T(8,128)}, f32[512,1024]{1,0:T(8,128)}), (f32[1024,512]{1,0:T(8,128)}, f32[1024,512]{1,0:T(8,128)}, f32[2,1024,32]{1,2,0:T(8,128)}, ...) | async-done | bytes 6553616 | tf_op jit(solution)/shard_map/psum | solution.py:284
  (576 shorter events, 309.2 us)
Async XLA Ops:
  7.2 151.7 %copy-start = (bf16[512,1024]{1,0:T(8,128)(2,1)S(1)}, bf16[512,1024]{1,0:T(8,128)(2,1)}, u32[]{:S(2)}) copy-start(bf16[512,1024]{1,0:T(8,128)(2,1)} %param.41) | copy-start | bytes 3145732
  7.2 129.4 %all-gather.9.cloned.1.call-start = ((), (), s32[]{:S(2)}) async-start(), calls=%async_computation.4 | async-start | bytes 2621440 | tf_op jit(solution)/shard_map/all_gather | solution.py:20
  15.3 9.9 %copy-start.85 = (f32[4,512]{1,0:T(4,128)S(1)}, f32[4,512]{1,0:T(4,128)}, u32[]{:S(2)}) copy-start(f32[4,512]{1,0:T(4,128)} %param.33) | copy-start | bytes 24580
  15.3 10.0 %copy-start.86 = (f32[4,2,32]{2,1,0:T(2,128)S(1)}, f32[4,2,32]{2,1,0:T(2,128)}, u32[]{:S(2)}) copy-start(f32[4,2,32]{2,1,0:T(2,128)} %param.34) | copy-start | bytes 3076
  15.3 10.1 %copy-start.95 = (f32[2,32]{1,0:T(2,128)S(1)}, f32[2,32]{1,0:T(2,128)}, u32[]{:S(2)}) copy-start(f32[2,32]{1,0:T(2,128)} %param.36) | copy-start | bytes 772
  19.7 11.4 %collective-permute-start = (bf16[2,3,576]{1,2,0:T(8,128)(2,1)}, bf16[2,3,576]{1,2,0:T(8,128)(2,1)}, u32[]{:S(2)}, u32[]{:S(2)}) collective-permute-start(bf16[2,3,576]{1,2,0:T(8,128)(2,1)} %pad_maximum_fusion.2), channel_id=1, source_target_pairs={{0,8},{8,16},{16,24},{1,9},{9,17},{17,25},{2,10},{10,18},{18,26},{... | collective-permute-start | bytes 20744 | tf_op jit(solution)/shard_map/ppermute | solution.py:13
  98.5 143.9 %all-gather.11.cloned.1.call-start = ((), (), s32[]{:S(2)}) async-start(), calls=%async_computation.5 | async-start | bytes 2621440 | tf_op jit(solution)/shard_map/all_gather | solution.py:20
  144.6 14.3 %copy-start.87 = (f32[512]{0:T(512)S(1)}, f32[512]{0:T(512)}, u32[]{:S(2)}) copy-start(f32[512]{0:T(512)} %param.40) | copy-start | bytes 6148
  158.9 14.5 %copy-start.74 = (f32[1024]{0:T(1024)}, f32[1024]{0:T(1024)S(1)}, u32[]{:S(2)}) copy-start(f32[1024]{0:T(1024)S(1)} %get-tuple-element.2072) | copy-start | bytes 12292
  186.7 260.5 %all-reduce.14.cloned.1.call-start = ((), (), s32[]{:S(2)}) async-start(), calls=%async_computation.6 | async-start | bytes 2097152
  203.7 8.2 copy-start.19
  225.2 8.3 copy-start.19
  287.8 15.4 %copy-start.82 = (f32[8]{0:T(128)S(1)}, f32[8]{0:T(128)}, u32[]{:S(2)}) copy-start(f32[8]{0:T(128)} %get-tuple-element.2823) | copy-start | bytes 100 | tf_op jit(solution)/shard_map/transpose(jvp(vmap()))/while
  303.2 9.5 %copy-start.83 = (f32[8]{0:T(128)}, f32[8]{0:T(128)S(1)}, u32[]{:S(2)}) copy-start(f32[8]{0:T(128)S(1)} %fusion.287) | copy-start | bytes 100 | tf_op jit(solution)/shard_map/transpose(jvp(vmap()))/while
  304.0 8.7 copy-start.8
  304.0 10.5 %copy-start.9 = (f32[2,256,8,64]{1,3,2,0:T(8,128)S(1)}, f32[2,256,8,64]{1,3,2,0:T(8,128)}, u32[]{:S(2)}) copy-start(f32[2,256,8,64]{1,3,2,0:T(8,128)} %get-tuple-element.2616) | copy-start | bytes 3145732 | tf_op jit(solution)/shard_map/transpose(jvp(vmap()))/while
  307.0 7.5 copy-start.41
  356.5 15.3 %copy-start.82 = (f32[8]{0:T(128)S(1)}, f32[8]{0:T(128)}, u32[]{:S(2)}) copy-start(f32[8]{0:T(128)} %get-tuple-element.2823) | copy-start | bytes 100 | tf_op jit(solution)/shard_map/transpose(jvp(vmap()))/while
  371.9 9.5 %copy-start.83 = (f32[8]{0:T(128)}, f32[8]{0:T(128)S(1)}, u32[]{:S(2)}) copy-start(f32[8]{0:T(128)S(1)} %fusion.287) | copy-start | bytes 100 | tf_op jit(solution)/shard_map/transpose(jvp(vmap()))/while
  372.7 8.7 copy-start.8
  372.7 10.5 %copy-start.9 = (f32[2,256,8,64]{1,3,2,0:T(8,128)S(1)}, f32[2,256,8,64]{1,3,2,0:T(8,128)}, u32[]{:S(2)}) copy-start(f32[2,256,8,64]{1,3,2,0:T(8,128)} %get-tuple-element.2616) | copy-start | bytes 3145732 | tf_op jit(solution)/shard_map/transpose(jvp(vmap()))/while
  375.7 7.5 copy-start.41
  375.7 7.5 copy-start.1
  396.5 129.5 %reduce-scatter.2.cloned.1.call-start = ((), (), s32[]{:S(2)}) async-start(), calls=%async_computation.1 | async-start | bytes 5242880 | tf_op jit(solution)/shard_map/reduce_scatter | solution.py:181
  401.5 161.9 %all-reduce.18.cloned.1.call-start = ((), (), s32[]{:S(2)}) async-start(), calls=%async_computation.8 | async-start | bytes 13107200 | tf_op jit(solution)/shard_map/psum | solution.py:285
  458.8 5.8 collective-permute-start.1
  476.0 245.7 %all-reduce.12.cloned.1.call-start = ((), (), s32[]{:S(2)}) async-start(), calls=%async_computation.3 | async-start | bytes 8388608 | tf_op jit(solution)/shard_map/psum | solution.py:271
  488.3 280.3 %all-gather.7.cloned.1.call-start = ((), (), s32[]{:S(2)}) async-start(), calls=%async_computation.2 | async-start | bytes 2621440 | tf_op jit(solution)/shard_map/all_gather | solution.py:190
  528.5 385.2 %all-reduce.16.cloned.1.call-start = ((), (), s32[]{:S(2)}) async-start(), calls=%async_computation.7 | async-start | bytes 13107200 | tf_op jit(solution)/shard_map/psum | solution.py:284
  564.0 157.7 %copy-start.59 = (f32[1024]{0:T(1024)S(1)}, f32[1024]{0:T(1024)}, u32[]{:S(2)}) copy-start(f32[1024]{0:T(1024)} %param.28) | copy-start | bytes 12292
  566.3 159.0 %copy-start.73 = (f32[8]{0:T(128)S(1)}, f32[8]{0:T(128)}, u32[]{:S(2)}) copy-start(f32[8]{0:T(128)} %get-tuple-element.1204) | copy-start | bytes 100
  566.3 159.0 %copy-start.89 = (f32[512]{0:T(512)S(1)}, f32[512]{0:T(512)}, u32[]{:S(2)}) copy-start(f32[512]{0:T(512)} %get-tuple-element.1850) | copy-start | bytes 6148
  (118 other events, 449.7 us)
Sparse Core Ops, SparseCore 0:
  98.6 37.9 all-gather.8
  186.8 40.1 all-gather.10
  396.6 50.5 all-reduce.13
  449.9 76.0 reduce-scatter.1
  529.8 33.4 all-reduce.17
  565.5 156.1 all-reduce.11
  723.9 44.6 all-gather.6
  772.4 141.3 all-reduce.15
